TPU v7x, 32 devices: a whole 2x2x4 slice. The times are simulated.
32 devices in a mesh: leaf: 32 (over z, y, x, core).
Axes of the slice: x: 2, y: 2, z: 4, core: 2. Of those that a mesh axis runs over, the one named last changes fastest.
Arguments:
- random_block: bfloat16 [16384, 256], P('leaf'), may hold values from -6 to 6
- diag_block: bfloat16 [16384, 512], P('leaf'), may hold values from -0.25 to 0.25
- basis_out: bfloat16 [16384, 256], P('leaf'), may hold values from -0.1875 to 0.1875
- basis_in: bfloat16 [16384, 256], P('leaf'), may hold values from -0.25 to 0.25
- low_up: bfloat16 [32, 2, 256, 256], P('leaf'), as said below
- low_down: bfloat16 [32, 2, 256, 256], P('leaf'), as said below
- low_coupling: bfloat16 [32, 2, 256, 256], P('leaf'), as said below
- top_up: bfloat16 [12, 256, 256], replicated, may hold values from -0.25 to 0.25
- top_down: bfloat16 [12, 256, 256], replicated, may hold values from -0.375 to 0.375
- top_coupling: bfloat16 [14, 256, 256], replicated, may hold values from -0.375 to 0.375
Outputs:
- sample: bfloat16 [16384, 256], P('leaf')
Inputs may be any that keep to these rules, and one draw needn't show every extreme that they name: `low_up`: for every level l below 2, entries [i, l] and [j, l] are the same matrix when i // 2^l == j // 2^l. `low_down`: for every level l below 2, entries [i, l] and [j, l] are the same matrix when i // 2^l == j // 2^l. `low_coupling`: for every level l below 2, entries [i, l] and [j, l] are the same matrix when i // 2^l == j // 2^l.
All inputs are finite; a program needn't handle non-finite values.
Results may differ from a plain program's by a relative error of at most 0.018.
Values may be sent and summed in bfloat16 or wider, within the bound.
A program may use at most 64 MiB of HBM per device.

v0:
```python
import jax
import jax.numpy as jnp
from jax import lax
from jax.sharding import PartitionSpec as P

TOP = 3


def as_sent(x):
    return jax.tree.map(lambda a: a.astype(jnp.bfloat16) if a.dtype == jnp.float32 else a, x)


def swapped(block, axis, stride):
    count = lax.axis_size(axis)
    route = []
    for low in range(count):
        high = low | 1 << stride
        if high != low and high < count:
            route += [(low, high), (high, low)]
    return lax.ppermute(block, axis, route)


def apply_left(matrix, values):
    return jnp.dot(matrix, values, preferred_element_type=jnp.float32)


def apply_trans(matrix, values):
    return lax.dot_general(
        matrix, values, (((0,), (0,)), ((), ())), preferred_element_type=jnp.float32
    )


def exchange_sibling(payload, height):
    return jax.tree.map(
        lambda part, own: part.astype(own.dtype), swapped(as_sent(payload), "leaf", height), payload
    )


def pick_node(table, position):
    return lax.dynamic_index_in_dim(table, position, 0, keepdims=False)


def per_device(
    random_block,
    diag_block,
    basis_out,
    basis_in,
    low_up,
    low_down,
    low_coupling,
    top_up,
    top_down,
    top_coupling,
):
    low_levels = low_up.shape[1]
    device = lax.axis_index("leaf")
    current = apply_trans(basis_in, random_block)
    lower_terms = []
    for height in range(low_levels):
        rounded = current.astype(jnp.bfloat16)
        lifted = apply_trans(low_up[0, height], rounded).astype(jnp.bfloat16)
        sibling_state, sibling_lift = exchange_sibling((rounded, lifted), height)
        lower_terms.append(apply_left(low_coupling[0, height], sibling_state))
        current = lifted.astype(jnp.float32) + sibling_lift.astype(jnp.float32)
    upper_terms = []
    for section in range(TOP):
        height = low_levels + section
        offset = 2 ** (TOP + 1) - 2 ** (TOP + 1 - section)
        own_node = jnp.right_shift(device, height)
        rounded = current.astype(jnp.bfloat16)
        coupler = pick_node(top_coupling, offset + own_node)
        if section < TOP - 1:
            lifter = pick_node(top_up, offset + own_node)
            lifted = apply_trans(lifter, rounded).astype(jnp.bfloat16)
            sibling_state, sibling_lift = exchange_sibling((rounded, lifted), height)
            current = lifted.astype(jnp.float32) + sibling_lift.astype(jnp.float32)
        else:
            (sibling_state,) = exchange_sibling((rounded,), height)
        upper_terms.append(apply_left(coupler, sibling_state))
    descent = upper_terms[-1]
    for section in range(TOP - 2, -1, -1):
        height = low_levels + section
        offset = 2 ** (TOP + 1) - 2 ** (TOP + 1 - section)
        own_node = jnp.right_shift(device, height)
        lowering = pick_node(top_down, offset + own_node)
        descent = apply_left(lowering, descent.astype(jnp.bfloat16)) + upper_terms[section]
    for height in range(low_levels - 1, -1, -1):
        descent = (
            apply_left(low_down[0, height], descent.astype(jnp.bfloat16)) + lower_terms[height]
        )
    local = apply_left(diag_block, random_block)
    spread = apply_left(basis_out, descent.astype(jnp.bfloat16))
    return (local + spread).astype(jnp.bfloat16)


def solution(mesh):
    placed = (
        P("leaf", None),
        P("leaf", None),
        P("leaf", None),
        P("leaf", None),
        P("leaf", None, None, None),
        P("leaf", None, None, None),
        P("leaf", None, None, None),
        P(),
        P(),
        P(),
    )
    return jax.shard_map(
        per_device, mesh=mesh, in_specs=placed, out_specs=P("leaf", None), check_vma=False
    )
```

profile of v0, /device:TPU:0, one launch (start us, length us, event | category | flops | bytes accessed | tf_op | source)
XLA Modules:
  0.0 43.7 jit_solution(3052125624222203056)
XLA Ops:
  0.0 0.0 copy-start
  0.0 1.4 %convolution_convert_fusion = bf16[256,256]{1,0:T(8,128)(2,1)S(1)} fusion(bf16[512,256]{1,0:T(8,128)(2,1)} %param.13, bf16[512,256]{1,0:T(8,128)(2,1)} %param.10), kind=kOutput, calls=%fused_computation.11 | convolution fusion | flops 67174400 | bytes 655360 | tf_op jit(solution)/shard_map/dot_general | solution.py:28
  1.5 1.1 %fusion.9 = bf16[256,256]{0,1:T(8,128)(2,1)S(1)} fusion(bf16[256,256]{1,0:T(8,128)(2,1)S(1)} %convolution_convert_fusion, bf16[1,2,256,256]{3,2,1,0:T(8,128)(2,1)} %param.14), kind=kOutput, calls=%fused_computation.20 | convolution fusion | flops 33619968 | bytes 393216 | tf_op jit(solution)/shard_map/dot_general | solution.py:28
  2.6 0.6 %collective-permute-start = (bf16[256,256]{0,1:T(8,128)(2,1)S(1)}, bf16[256,256]{0,1:T(8,128)(2,1)S(1)}, u32[]{:S(2)}, u32[]{:S(2)}) collective-permute-start(bf16[256,256]{0,1:T(8,128)(2,1)S(1)} %fusion.9), channel_id=1, source_target_pairs={{0,1},{1,0},{2,3},{3,2},{4,5},{5,4},{6,7},{7,6},{8,9},{9,8},{10,11... | collective-permute-start | bytes 393224 | tf_op jit(solution)/shard_map/ppermute | solution.py:20
  3.2 1.0 %collective-permute-done = bf16[256,256]{0,1:T(8,128)(2,1)S(1)} collective-permute-done((bf16[256,256]{0,1:T(8,128)(2,1)S(1)}, bf16[256,256]{0,1:T(8,128)(2,1)S(1)}, u32[]{:S(2)}, u32[]{:S(2)}) %collective-permute-start) | collective-permute-done | bytes 131104 | tf_op jit(solution)/shard_map/ppermute | solution.py:20
  4.2 1.1 %fusion.10 = bf16[256,256]{0,1:T(8,128)(2,1)S(1)} fusion(bf16[256,256]{0,1:T(8,128)(2,1)S(1)} %add_convert_fusion.3, bf16[1,2,256,256]{3,2,1,0:T(8,128)(2,1)} %param.14), kind=kOutput, calls=%fused_computation.21 | convolution fusion | flops 33619968 | bytes 393216 | tf_op jit(solution)/shard_map/dot_general | solution.py:28
  5.3 2.9 %collective-permute-start.1 = (bf16[256,256]{0,1:T(8,128)(2,1)S(1)}, bf16[256,256]{0,1:T(8,128)(2,1)S(1)}, u32[]{:S(2)}, u32[]{:S(2)}) collective-permute-start(bf16[256,256]{0,1:T(8,128)(2,1)S(1)} %fusion.10), channel_id=1, source_target_pairs={{0,2},{2,0},{1,3},{3,1},{4,6},{6,4},{5,7},{7,5},{8,10},{10,8},{9,1... | collective-permute-start | bytes 393224 | tf_op jit(solution)/shard_map/ppermute | solution.py:20
  8.2 3.8 %collective-permute-done.1 = bf16[256,256]{0,1:T(8,128)(2,1)S(1)} collective-permute-done((bf16[256,256]{0,1:T(8,128)(2,1)S(1)}, bf16[256,256]{0,1:T(8,128)(2,1)S(1)}, u32[]{:S(2)}, u32[]{:S(2)}) %collective-permute-start.1) | collective-permute-done | bytes 131104 | tf_op jit(solution)/shard_map/ppermute | solution.py:20
  12.0 1.1 %convolution_convert_fusion.3 = bf16[256,256]{1,0:T(8,128)(2,1)S(1)} fusion(bf16[256,256]{0,1:T(8,128)(2,1)S(1)} %add_convert_fusion.2, bf16[12,256,256]{2,1,0:T(8,128)(2,1)} %param.17, s32[]{:T(128)S(6)} %select_n.19), kind=kOutput, calls=%fused_computation.14 | convolution fusion | flops 33619968 | bytes 393220 | tf_op jit(solution)/shard_map/dot_general | solution.py:28
  13.2 1.8 %collective-permute-start.2 = (bf16[256,256]{1,0:T(8,128)(2,1)S(1)}, bf16[256,256]{1,0:T(8,128)(2,1)S(1)}, u32[]{:S(2)}, u32[]{:S(2)}) collective-permute-start(bf16[256,256]{1,0:T(8,128)(2,1)S(1)} %convolution_convert_fusion.3), channel_id=1, source_target_pairs={{0,4},{4,0},{1,5},{5,1},{2,6},{6,2},{3,7},{7,3},{8,12},{12,8},{9,1... | collective-permute-start | bytes 393224 | tf_op jit(solution)/shard_map/ppermute | solution.py:20
  15.0 3.2 %collective-permute-done.2 = bf16[256,256]{1,0:T(8,128)(2,1)S(1)} collective-permute-done((bf16[256,256]{1,0:T(8,128)(2,1)S(1)}, bf16[256,256]{1,0:T(8,128)(2,1)S(1)}, u32[]{:S(2)}, u32[]{:S(2)}) %collective-permute-start.2) | collective-permute-done | bytes 131104 | tf_op jit(solution)/shard_map/ppermute | solution.py:20
  18.2 1.1 %convolution_convert_fusion.2 = bf16[256,256]{1,0:T(8,128)(2,1)S(1)} fusion(bf16[256,256]{1,0:T(8,128)(2,1)S(1)} %add_convert_fusion.1, bf16[12,256,256]{2,1,0:T(8,128)(2,1)} %param.17, s32[]{:T(128)S(6)} %select_n.20), kind=kOutput, calls=%fused_computation.13 | convolution fusion | flops 33619968 | bytes 393220 | tf_op jit(solution)/shard_map/dot_general | solution.py:28
  19.4 1.9 %collective-permute-start.3 = (bf16[256,256]{1,0:T(8,128)(2,1)S(1)}, bf16[256,256]{1,0:T(8,128)(2,1)S(1)}, u32[]{:S(2)}, u32[]{:S(2)}) collective-permute-start(bf16[256,256]{1,0:T(8,128)(2,1)S(1)} %convolution_convert_fusion.2), channel_id=1, source_target_pairs={{0,8},{8,0},{1,9},{9,1},{2,10},{10,2},{3,11},{11,3},{4,12},{12,4},... | collective-permute-start | bytes 393224 | tf_op jit(solution)/shard_map/ppermute | solution.py:20
  21.3 0.0 collective-permute-start.8
  21.3 3.1 %collective-permute-done.3 = bf16[256,256]{1,0:T(8,128)(2,1)S(1)} collective-permute-done((bf16[256,256]{1,0:T(8,128)(2,1)S(1)}, bf16[256,256]{1,0:T(8,128)(2,1)S(1)}, u32[]{:S(2)}, u32[]{:S(2)}) %collective-permute-start.3) | collective-permute-done | bytes 131104 | tf_op jit(solution)/shard_map/ppermute | solution.py:20
  24.4 3.3 %collective-permute-start.4 = (bf16[256,256]{1,0:T(8,128)(2,1)S(1)}, bf16[256,256]{1,0:T(8,128)(2,1)S(1)}, u32[]{:S(2)}, u32[]{:S(2)}) collective-permute-start(bf16[256,256]{1,0:T(8,128)(2,1)S(1)} %add_convert_fusion), channel_id=1, source_target_pairs={{0,16},{16,0},{1,17},{17,1},{2,18},{18,2},{3,19},{19,3},{4,20},{20... | collective-permute-start | bytes 393224 | tf_op jit(solution)/shard_map/ppermute | solution.py:20
  27.8 0.0 copy-done.1
  27.8 1.3 %fusion.56 = f32[512,256]{1,0:T(8,128)S(1)} fusion(bf16[512,512]{1,0:T(8,128)(2,1)} %param.11, bf16[512,256]{1,0:T(8,128)(2,1)S(1)} %copy-done.1), kind=kOutput, calls=%fused_computation.58 | convolution fusion | flops 134217728 | bytes 1310720 | tf_op jit(solution)/shard_map/dot_general | solution.py:24
  29.1 1.6 %collective-permute-start.7 = (bf16[256,256]{0,1:T(8,128)(2,1)S(1)}, bf16[256,256]{0,1:T(8,128)(2,1)}, u32[]{:S(2)}, u32[]{:S(2)}) collective-permute-start(bf16[256,256]{0,1:T(8,128)(2,1)S(1)} %add_convert_fusion.3), channel_id=1, source_target_pairs={{0,2},{2,0},{1,3},{3,1},{4,6},{6,4},{5,7},{7,5},{8,10},{10,8},{9,1... | collective-permute-start | bytes 393224 | tf_op jit(solution)/shard_map/ppermute | solution.py:20
  30.7 1.5 %collective-permute-start.6 = (bf16[256,256]{0,1:T(8,128)(2,1)S(1)}, bf16[256,256]{0,1:T(8,128)(2,1)}, u32[]{:S(2)}, u32[]{:S(2)}) collective-permute-start(bf16[256,256]{0,1:T(8,128)(2,1)S(1)} %add_convert_fusion.2), channel_id=1, source_target_pairs={{0,4},{4,0},{1,5},{5,1},{2,6},{6,2},{3,7},{7,3},{8,12},{12,8},{9,1... | collective-permute-start | bytes 393224 | tf_op jit(solution)/shard_map/ppermute | solution.py:20
  32.2 1.1 %collective-permute-start.5 = (bf16[256,256]{1,0:T(8,128)(2,1)S(1)}, bf16[256,256]{1,0:T(8,128)(2,1)}, u32[]{:S(2)}, u32[]{:S(2)}) collective-permute-start(bf16[256,256]{1,0:T(8,128)(2,1)S(1)} %add_convert_fusion.1), channel_id=1, source_target_pairs={{0,8},{8,0},{1,9},{9,1},{2,10},{10,2},{3,11},{11,3},{4,12},{12,4},... | collective-permute-start | bytes 393224 | tf_op jit(solution)/shard_map/ppermute | solution.py:20
  33.3 0.0 collective-permute-done.4
  33.3 0.0 copy-done
  33.3 1.3 %fusion.11 = f32[256,256]{1,0:T(8,128)S(1)} fusion(bf16[256,256]{1,0:T(8,128)(2,1)S(1)} %collective-permute-done.4, bf16[14,256,256]{2,1,0:T(8,128)(2,1)S(1)} %copy-done, s32[]{:T(128)S(6)} %select_n.21, bf16[12,256,256]{2,1,0:T(8,128)(2,1)} %param.18, s32[]{:T(128)S(6)} %select_n.20), kind=kOutput, calls=%fused_computation.22 | convolution fusion | flops 67174400 | bytes 655368 | tf_op jit(solution)/shard_map/dot_general | solution.py:24
  34.6 2.6 %collective-permute-done.5 = bf16[256,256]{1,0:T(8,128)(2,1)} collective-permute-done((bf16[256,256]{1,0:T(8,128)(2,1)S(1)}, bf16[256,256]{1,0:T(8,128)(2,1)}, u32[]{:S(2)}, u32[]{:S(2)}) %collective-permute-start.5) | collective-permute-done | bytes 131104 | tf_op jit(solution)/shard_map/ppermute | solution.py:20
  37.3 1.4 %fusion.8 = f32[256,256]{1,0:T(8,128)S(1)} fusion(f32[256,256]{1,0:T(8,128)S(1)} %fusion.11, bf16[256,256]{1,0:T(8,128)(2,1)} %collective-permute-done.5, bf16[14,256,256]{2,1,0:T(8,128)(2,1)S(1)} %copy-done, s32[]{:T(128)S(6)} %select_n.22, bf16[12,256,256]{2,1,0:T(8,128)(2,1)} %param.18, s32[]{:T(128)S(6)} %select_n.19), kind=kOutput, calls=%fused_computation.19 | convolution fusion | flops 67239936 | bytes 917512 | tf_op jit(solution)/shard_map/dot_general | solution.py:24
  38.6 0.0 collective-permute-done.6
  38.6 1.4 %fusion.7 = f32[256,256]{1,0:T(8,128)S(1)} fusion(f32[256,256]{1,0:T(8,128)S(1)} %fusion.8, bf16[256,256]{0,1:T(8,128)(2,1)} %collective-permute-done.6, bf16[1,2,256,256]{3,2,1,0:T(8,128)(2,1)} %param.15, bf16[14,256,256]{2,1,0:T(8,128)(2,1)S(1)} %copy-done, s32[]{:T(128)S(6)} %select_n.23), kind=kOutput, calls=%fused_computation.18 | convolution fusion | flops 67239936 | bytes 917508 | tf_op jit(solution)/shard_map/dot_general | solution.py:24
  40.1 0.0 collective-permute-done.7
  40.1 1.4 %fusion.6 = f32[256,256]{1,0:T(8,128)S(1)} fusion(f32[256,256]{1,0:T(8,128)S(1)} %fusion.7, bf16[256,256]{0,1:T(8,128)(2,1)} %collective-permute-done.7, bf16[1,2,256,256]{3,2,1,0:T(8,128)(2,1)} %param.15, bf16[1,2,256,256]{3,2,1,0:T(8,128)(2,1)} %param.16), kind=kOutput, calls=%fused_computation.17 | convolution fusion | flops 67239936 | bytes 917504 | tf_op jit(solution)/shard_map/dot_general | solution.py:24
  41.5 0.0 collective-permute-done.8
  41.5 2.2 %fusion.1 = bf16[512,256]{1,0:T(8,128)(2,1)} fusion(f32[512,256]{1,0:T(8,128)S(1)} %fusion.56, bf16[512,256]{1,0:T(8,128)(2,1)} %param.12, f32[256,256]{1,0:T(8,128)S(1)} %fusion.6, bf16[256,256]{1,0:T(8,128)(2,1)S(1)} %collective-permute-done.8, bf16[1,2,256,256]{3,2,1,0:T(8,128)(2,1)} %param.16), kind=kOutput, calls=%fused_computation.2 | convolution fusion | flops 101056512 | bytes 1572864 | tf_op jit(solution)/shard_map/dot_general | solution.py:24
  (5 shorter events, 0.1 us)
Async XLA Ops:
  0.0 33.3 %copy-start = (bf16[14,256,256]{2,1,0:T(8,128)(2,1)S(1)}, bf16[14,256,256]{2,1,0:T(8,128)(2,1)}, u32[]{:S(2)}) copy-start(bf16[14,256,256]{2,1,0:T(8,128)(2,1)} %param.19) | copy-start | bytes 5505028
  0.0 27.8 %copy-start.1 = (bf16[512,256]{1,0:T(8,128)(2,1)S(1)}, bf16[512,256]{1,0:T(8,128)(2,1)}, u32[]{:S(2)}) copy-start(bf16[512,256]{1,0:T(8,128)(2,1)} %param.10) | copy-start | bytes 786436
  2.6 1.5 %collective-permute-start = (bf16[256,256]{0,1:T(8,128)(2,1)S(1)}, bf16[256,256]{0,1:T(8,128)(2,1)S(1)}, u32[]{:S(2)}, u32[]{:S(2)}) collective-permute-start(bf16[256,256]{0,1:T(8,128)(2,1)S(1)} %fusion.9), channel_id=1, source_target_pairs={{0,1},{1,0},{2,3},{3,2},{4,5},{5,4},{6,7},{7,6},{8,9},{9,8},{10,11... | collective-permute-start | bytes 393224 | tf_op jit(solution)/shard_map/ppermute | solution.py:20
  5.3 6.7 %collective-permute-start.1 = (bf16[256,256]{0,1:T(8,128)(2,1)S(1)}, bf16[256,256]{0,1:T(8,128)(2,1)S(1)}, u32[]{:S(2)}, u32[]{:S(2)}) collective-permute-start(bf16[256,256]{0,1:T(8,128)(2,1)S(1)} %fusion.10), channel_id=1, source_target_pairs={{0,2},{2,0},{1,3},{3,1},{4,6},{6,4},{5,7},{7,5},{8,10},{10,8},{9,1... | collective-permute-start | bytes 393224 | tf_op jit(solution)/shard_map/ppermute | solution.py:20
  13.2 5.0 %collective-permute-start.2 = (bf16[256,256]{1,0:T(8,128)(2,1)S(1)}, bf16[256,256]{1,0:T(8,128)(2,1)S(1)}, u32[]{:S(2)}, u32[]{:S(2)}) collective-permute-start(bf16[256,256]{1,0:T(8,128)(2,1)S(1)} %convolution_convert_fusion.3), channel_id=1, source_target_pairs={{0,4},{4,0},{1,5},{5,1},{2,6},{6,2},{3,7},{7,3},{8,12},{12,8},{9,1... | collective-permute-start | bytes 393224 | tf_op jit(solution)/shard_map/ppermute | solution.py:20
  19.4 5.0 %collective-permute-start.3 = (bf16[256,256]{1,0:T(8,128)(2,1)S(1)}, bf16[256,256]{1,0:T(8,128)(2,1)S(1)}, u32[]{:S(2)}, u32[]{:S(2)}) collective-permute-start(bf16[256,256]{1,0:T(8,128)(2,1)S(1)} %convolution_convert_fusion.2), channel_id=1, source_target_pairs={{0,8},{8,0},{1,9},{9,1},{2,10},{10,2},{3,11},{11,3},{4,12},{12,4},... | collective-permute-start | bytes 393224 | tf_op jit(solution)/shard_map/ppermute | solution.py:20
  21.3 20.2 %collective-permute-start.8 = (bf16[256,256]{1,0:T(8,128)(2,1)S(1)}, bf16[256,256]{1,0:T(8,128)(2,1)S(1)}, u32[]{:S(2)}, u32[]{:S(2)}) collective-permute-start(bf16[256,256]{1,0:T(8,128)(2,1)S(1)} %convolution_convert_fusion), channel_id=1, source_target_pairs={{0,1},{1,0},{2,3},{3,2},{4,5},{5,4},{6,7},{7,6},{8,9},{9,8},{10,11... | collective-permute-start | bytes 393224 | tf_op jit(solution)/shard_map/ppermute | solution.py:20
  24.4 8.9 %collective-permute-start.4 = (bf16[256,256]{1,0:T(8,128)(2,1)S(1)}, bf16[256,256]{1,0:T(8,128)(2,1)S(1)}, u32[]{:S(2)}, u32[]{:S(2)}) collective-permute-start(bf16[256,256]{1,0:T(8,128)(2,1)S(1)} %add_convert_fusion), channel_id=1, source_target_pairs={{0,16},{16,0},{1,17},{17,1},{2,18},{18,2},{3,19},{19,3},{4,20},{20... | collective-permute-start | bytes 393224 | tf_op jit(solution)/shard_map/ppermute | solution.py:20
  29.1 11.0 %collective-permute-start.7 = (bf16[256,256]{0,1:T(8,128)(2,1)S(1)}, bf16[256,256]{0,1:T(8,128)(2,1)}, u32[]{:S(2)}, u32[]{:S(2)}) collective-permute-start(bf16[256,256]{0,1:T(8,128)(2,1)S(1)} %add_convert_fusion.3), channel_id=1, source_target_pairs={{0,2},{2,0},{1,3},{3,1},{4,6},{6,4},{5,7},{7,5},{8,10},{10,8},{9,1... | collective-permute-start | bytes 393224 | tf_op jit(solution)/shard_map/ppermute | solution.py:20
  30.7 8.0 %collective-permute-start.6 = (bf16[256,256]{0,1:T(8,128)(2,1)S(1)}, bf16[256,256]{0,1:T(8,128)(2,1)}, u32[]{:S(2)}, u32[]{:S(2)}) collective-permute-start(bf16[256,256]{0,1:T(8,128)(2,1)S(1)} %add_convert_fusion.2), channel_id=1, source_target_pairs={{0,4},{4,0},{1,5},{5,1},{2,6},{6,2},{3,7},{7,3},{8,12},{12,8},{9,1... | collective-permute-start | bytes 393224 | tf_op jit(solution)/shard_map/ppermute | solution.py:20
  32.2 5.1 %collective-permute-start.5 = (bf16[256,256]{1,0:T(8,128)(2,1)S(1)}, bf16[256,256]{1,0:T(8,128)(2,1)}, u32[]{:S(2)}, u32[]{:S(2)}) collective-permute-start(bf16[256,256]{1,0:T(8,128)(2,1)S(1)} %add_convert_fusion.1), channel_id=1, source_target_pairs={{0,8},{8,0},{1,9},{9,1},{2,10},{10,2},{3,11},{11,3},{4,12},{12,4},... | collective-permute-start | bytes 393224 | tf_op jit(solution)/shard_map/ppermute | solution.py:20
where the time goes:
time: 44.1 us; the launch traced here: 43.7 us
  matrix products  14.9 us (34%)
  starting transfers between devices  14.7 us (33%)
  waiting for transfers between devices  13.8 us (31%)
    ppermute x9, starting transfers between devices, swapped(): return lax.ppermute(block, axis, route)  14.7 us
    ppermute x9, waiting for transfers between devices, swapped(): return lax.ppermute(block, axis, route)  13.8 us
    dot_general x6, matrix products, apply_left(): return jnp.dot(matrix, values, preferred_element_type=jnp.float32)  9.02 us
    dot_general x5, matrix products, apply_trans(): lax.dot_general(matrix, values, (((0,), (0,)), ((), ())), preferred_eleme...  5.92 us
  transfers between devices with their start and end apart: 9, of which 5 were waited for; matrix products, arithmetic and copies ran while one was open for 16% of the time, Pallas kernels for 0%

commit v1 on v0

v1 whole, which is shorter than its diff:
```python
import functools

import jax
import jax.numpy as jnp
from jax import lax
from jax.experimental import pallas as pl
from jax.experimental.pallas import tpu as pltpu
from jax.sharding import PartitionSpec as P

TOP = 3
CHUNKS = 2
MESH = pl.DeviceIdType.MESH


def nn(a, b):
    return jnp.dot(a, b, preferred_element_type=jnp.float32)


def nt(a, b):
    return lax.dot_general(a, b, (((1,), (1,)), ((), ())), preferred_element_type=jnp.float32)


def tn(a, b):
    return lax.dot_general(a, b, (((0,), (0,)), ((), ())), preferred_element_type=jnp.float32)


def bf(a):
    return a.astype(jnp.bfloat16)


def f32(a):
    return a.astype(jnp.float32)


def kernel(levels, low, x, d, u, v, lup, ldn, lcp, tup, tdn, tcp, out,
           xs, dv, uv, vv, wv, wsib, rv, bv, cb0, rcb0, scb, rcb, slift, rlift, own, fl, f0, acc,
           zb1, rz1, in_sem, s0, r0, scs, rcs, sls, rls, szs, rzs):
    me = lax.axis_index("leaf")
    side = lax.rem(me, 2)
    half = xs.shape[2]
    step = half // CHUNKS

    def bit_partner(height):
        stride = 2 ** height
        bit = lax.rem(me // stride, 2)
        return me + stride - 2 * stride * bit

    partners = [bit_partner(height) for height in range(levels)]

    loads = []

    def load(src, dst):
        copy = pltpu.make_async_copy(src, dst, in_sem.at[len(loads)])
        copy.start()
        loads.append(copy)
        return copy

    def node(height):
        section = height - low
        return 2 ** (TOP + 1) - 2 ** (TOP + 1 - section) + me // 2 ** height

    def node_sib(height):
        section = height - low
        return 2 ** (TOP + 1) - 2 ** (TOP + 1 - section) + partners[height] // 2 ** height

    other_cols = pl.ds(pl.multiple_of((1 - side) * half, half), half)
    self_cols = pl.ds(pl.multiple_of(side * half, half), half)
    ld_v = load(v, vv)
    ld_xo = load(x.at[:, other_cols], xs.at[0])
    ld_w, ld_ws, ld_r, ld_b = {}, {}, {}, {}
    ld_w[0] = load(lup.at[0, 0], wv.at[0])
    ld_xs = load(x.at[:, self_cols], xs.at[1])

    barrier = pltpu.get_barrier_semaphore()
    for partner in partners:
        pl.semaphore_signal(barrier, inc=1, device_id=(partner,), device_id_type=MESH)

    for height in range(1, levels - 1):
        if height < low:
            ld_w[height] = load(lup.at[0, height], wv.at[height])
        else:
            ld_w[height] = load(tup.at[node(height)], wv.at[height])
            ld_ws[height] = load(tup.at[node_sib(height)], wsib.at[height - low])
    ld_d = load(d, dv)
    for height in range(levels):
        ld_b[height] = load(lcp.at[0, height] if height < low else tcp.at[node(height)], bv.at[height])
    for height in range(levels - 2, -1, -1):
        ld_r[height] = load(ldn.at[0, height] if height < low else tdn.at[node(height)], rv.at[height])
    ld_u = load(u, uv)

    sent = []

    def send(src, dst, ssem, rsem, partner):
        copy = pltpu.make_async_remote_copy(
            src_ref=src, dst_ref=dst, send_sem=ssem, recv_sem=rsem,
            device_id=(partner,), device_id_type=MESH,
        )
        copy.start()
        sent.append(copy)
        return copy

    ld_v.wait()
    ld_xo.wait()
    cb0[0] = bf(tn(xs[0], vv[...]))
    ld_w[0].wait()
    slift[0] = bf(nn(cb0[0], wv[0]))
    pl.semaphore_wait(barrier, levels)
    rl = {}
    rc = {}
    for k in range(CHUNKS):
        rows = pl.ds(k * step, step)
        rl[0, k] = send(slift.at[0, rows], rlift.at[0, rows], sls.at[0, k], rls.at[0, k], partners[0])
    ld_xs.wait()
    cb0[1] = bf(tn(xs[1], vv[...]))
    own[0] = bf(nn(cb0[1], wv[0]))
    rc0 = [send(cb0.at[j], rcb0.at[1 - j], s0.at[j], r0.at[j], partners[0]) for j in range(2)]

    for height in range(1, levels):
        if height < levels - 1:
            ld_w[height].wait()
        if height > low:
            ld_ws[height - 1].wait()
        for k in range(CHUNKS):
            rows = pl.ds(k * step, step)
            if height <= low:
                rl[height - 1, k].wait_recv()
                theirs = rlift[height - 1, rows]
            else:
                rc[height - 1, k].wait_recv()
                theirs = bf(nn(rcb[height - 1, rows], wsib[height - 1 - low]))
            c = f32(own[height - 1, rows]) + f32(theirs)
            scb[height, rows] = bf(c)
            if height < low:
                lifted = bf(nn(bf(c), wv[height]))
                slift[height, rows] = lifted
                own[height, rows] = lifted
                rl[height, k] = send(slift.at[height, rows], rlift.at[height, rows],
                                     sls.at[height, k], rls.at[height, k], partners[height])
            else:
                rc[height, k] = send(scb.at[height, rows], rcb.at[height, rows],
                                     scs.at[height, k], rcs.at[height, k], partners[height])
        if height < low:
            for k in range(CHUNKS):
                rows = pl.ds(k * step, step)
                rc[height, k] = send(scb.at[height, rows], rcb.at[height, rows],
                                     scs.at[height, k], rcs.at[height, k], partners[height])
        elif height < levels - 1:
            own[height] = bf(nn(scb[height], wv[height]))
        if height == 1:
            ld_d.wait()
            for j in range(2):
                acc[j] = nn(dv[...], xs[j])
        if height == 2:
            ld_b[0].wait()
            for j in range(2):
                rc0[1 - j].wait_recv()
                f0[j] = nt(rcb0[j], bv[0])
        if height > low:
            ld_b[height - 1].wait()
            fl[height - 1] = nt(rcb[height - 1], bv[height - 1])
        if height == levels - 1:
            for lower in range(1, low):
                ld_b[lower].wait()
                for k in range(CHUNKS):
                    rc[lower, k].wait_recv()
                fl[lower] = nt(rcb[lower], bv[lower])

    ld_b[levels - 1].wait()
    for height in range(levels - 2, -1, -1):
        ld_r[height].wait()
    ld_u.wait()
    rz = []
    for k in range(CHUNKS):
        rows = pl.ds(k * step, step)
        rc[levels - 1, k].wait_recv()
        z = nt(rcb[levels - 1, rows], bv[levels - 1])
        for height in range(levels - 2, 0, -1):
            z = nt(bf(z), rv[height]) + fl[height, rows]
        zb1[rows] = bf(z)
        rz.append(send(zb1.at[rows], rz1.at[rows], szs.at[k], rzs.at[k], partners[0]))
    z0 = nt(zb1[...], rv[0]) + f0[1]
    out[:, self_cols] = bf(acc[1] + nt(uv[...], bf(z0)))
    for copy in rz:
        copy.wait_recv()
    z0 = nt(rz1[...], rv[0]) + f0[0]
    out[:, other_cols] = bf(acc[0] + nt(uv[...], bf(z0)))
    for copy in sent:
        copy.wait_send()


def per_device(random_block, diag_block, basis_out, basis_in, low_up, low_down, low_coupling,
               top_up, top_down, top_coupling):
    levels = lax.axis_size("leaf").bit_length() - 1
    low = low_up.shape[1]
    leaf, ncol = random_block.shape
    rank = basis_in.shape[1]
    half = ncol // 2
    b16, f4 = jnp.bfloat16, jnp.float32
    dma = pltpu.SemaphoreType.DMA
    hbm = pl.BlockSpec(memory_space=pltpu.HBM)
    return pl.pallas_call(
        functools.partial(kernel, levels, low),
        out_shape=jax.ShapeDtypeStruct((leaf, ncol), b16),
        in_specs=[hbm] * 10,
        out_specs=pl.BlockSpec(memory_space=pltpu.VMEM),
        scratch_shapes=[
            pltpu.VMEM((2, leaf, half), b16),
            pltpu.VMEM((leaf, leaf), b16),
            pltpu.VMEM((leaf, rank), b16),
            pltpu.VMEM((leaf, rank), b16),
            pltpu.VMEM((levels - 1, rank, rank), b16),
            pltpu.VMEM((TOP - 1, rank, rank), b16),
            pltpu.VMEM((levels - 1, rank, rank), b16),
            pltpu.VMEM((levels, rank, rank), b16),
            pltpu.VMEM((2, half, rank), b16),
            pltpu.VMEM((2, half, rank), b16),
            pltpu.VMEM((levels, half, rank), b16),
            pltpu.VMEM((levels, half, rank), b16),
            pltpu.VMEM((low, half, rank), b16),
            pltpu.VMEM((low, half, rank), b16),
            pltpu.VMEM((levels - 1, half, rank), b16),
            pltpu.VMEM((levels - 1, half, rank), f4),
            pltpu.VMEM((2, half, rank), f4),
            pltpu.VMEM((2, leaf, half), f4),
            pltpu.VMEM((half, rank), b16),
            pltpu.VMEM((half, rank), b16),
            dma((4 * levels + 8,)),
            dma((2,)),
            dma((2,)),
            dma((levels, CHUNKS)),
            dma((levels, CHUNKS)),
            dma((low, CHUNKS)),
            dma((low, CHUNKS)),
            dma((CHUNKS,)),
            dma((CHUNKS,)),
        ],
        compiler_params=pltpu.CompilerParams(collective_id=0, has_side_effects=True),
    )(random_block, diag_block, basis_out, basis_in, low_up, low_down, low_coupling,
      top_up, top_down, top_coupling)


def solution(mesh):
    rows = P("leaf", None)
    gens = P("leaf", None, None, None)
    return jax.shard_map(
        per_device, mesh=mesh,
        in_specs=(rows, rows, rows, rows, gens, gens, gens, P(), P(), P()),
        out_specs=rows, check_vma=False,
    )
```

time: 44.1 us -> 25.1 us (0.57)
  Pallas kernels: 0 us -> 23.1 us
  matrix products: 14.9 us -> 0 us
  starting transfers between devices: 14.7 us -> 0 us
  waiting for transfers between devices: 13.8 us -> 0 us
  local copies, waits for them, and re-layouts: 0.01 us -> 1.67 us
    pallas_call x0 -> x1, Pallas kernels: none -> 23.1 us  [per_device(): pl.pallas_call(functools.partial(kernel, levels, low), out_shape=jax.Shap...]
    dot_general x11 -> x0, matrix products: 14.9 us -> none  [the longest x6 9.02 us: apply_left(): return jnp.dot(matrix, values, preferred_element_type=jnp.float32)]
    ppermute x9 -> x0, starting transfers between devices: 14.7 us -> none  [swapped(): return lax.ppermute(block, axis, route)]
    ppermute x9 -> x0, waiting for transfers between devices: 13.8 us -> none  [swapped(): return lax.ppermute(block, axis, route)]
    unnamed x4 -> x1, local copies, waits for them, and re-layouts: 0.01 us -> 1.67 us
  transfers between devices with their start and end apart: 9 -> 0, of which waited for: 5 -> 0; matrix products, arithmetic and copies ran while one was open for 16% -> 0% of each run, Pallas kernels for 0% -> 0%
where the time goes in v1:
time: 25.1 us; the launch traced here: 24.7 us
  Pallas kernels  23.1 us (92%)
  local copies, waits for them, and re-layouts  1.67 us (7%)
    pallas_call x1, Pallas kernels, per_device(): pl.pallas_call(functools.partial(kernel, levels, low), out_shape=jax.Shap...  23.1 us
    unnamed x1, local copies, waits for them, and re-layouts  1.67 us

profile of v1, /device:TPU:0, one launch (start us, length us, event | category | flops | bytes accessed | tf_op | source)
XLA Modules:
  0.0 24.7 jit_solution(762306422796157538)
XLA Ops:
  0.0 23.1 %shard_map.100 = bf16[512,256]{1,0:T(8,128)(2,1)} custom-call(bf16[512,256]{1,0:T(8,128)(2,1)} %x.1, bf16[512,512]{1,0:T(8,128)(2,1)} %d.1, bf16[512,256]{1,0:T(8,128)(2,1)} %u.1, bf16[512,256]{1,0:T(8,128)(2,1)} %v.1, bf16[1,2,256,256]{3,2,1,0:T(8,128)(2,1)} %lup.1, bf16[1,2,256,256]{3,2,1,0:T(8,128)(2,1)} %ldn.1, bf16[1,2,256,256]{3,2,1,0:T(8,128)(2,1)} %lcp.1, ...), custom_call_target="tpu_custom_call" | custom-call | tf_op jit(solution)/shard_map/pallas_call | solution.py:201
  23.1 1.7 %copy.12 = bf16[512,256]{1,0:T(8,128)(2,1)} copy(bf16[512,256]{1,0:T(8,128)(2,1)} %shard_map.100) | data formatting | bytes 524288

commit v2 on v1

--- a/solution.py
+++ b/solution.py
@@ -8,7 +8,7 @@
 from jax.sharding import PartitionSpec as P
 
 TOP = 3
-CHUNKS = 2
+CHUNKS = 4
 MESH = pl.DeviceIdType.MESH
 
 
@@ -34,7 +34,7 @@
 
 def kernel(levels, low, x, d, u, v, lup, ldn, lcp, tup, tdn, tcp, out,
            xs, dv, uv, vv, wv, wsib, rv, bv, cb0, rcb0, scb, rcb, slift, rlift, own, fl, f0, acc,
-           zb1, rz1, in_sem, s0, r0, scs, rcs, sls, rls, szs, rzs):
+           zb1, rz1, comp, path, zs, in_sem, s0, r0, scs, rcs, sls, rls, szs, rzs):
     me = lax.axis_index("leaf")
     side = lax.rem(me, 2)
     half = xs.shape[2]
@@ -150,11 +150,20 @@
             ld_d.wait()
             for j in range(2):
                 acc[j] = nn(dv[...], xs[j])
-        if height == 2:
+        if height == min(2, levels - 1):
             ld_b[0].wait()
             for j in range(2):
                 rc0[1 - j].wait_recv()
                 f0[j] = nt(rcb0[j], bv[0])
+        if height == min(3, levels - 1):
+            ld_b[levels - 1].wait()
+            for up in range(levels - 2, 0, -1):
+                ld_r[up].wait()
+                comp[...] = bf(nn(rv[up], bv[levels - 1] if up == levels - 2 else comp[...]))
+            ld_r[0].wait()
+            ld_u.wait()
+            path[...] = bf(nn(uv[...], rv[0]))
+            path[...] = bf(nn(path[...], comp[...]))
         if height > low:
             ld_b[height - 1].wait()
             fl[height - 1] = nt(rcb[height - 1], bv[height - 1])
@@ -164,26 +173,26 @@
                 for k in range(CHUNKS):
                     rc[lower, k].wait_recv()
                 fl[lower] = nt(rcb[lower], bv[lower])
-
-    ld_b[levels - 1].wait()
-    for height in range(levels - 2, -1, -1):
-        ld_r[height].wait()
-    ld_u.wait()
+            z = fl[levels - 2]
+            for up in range(levels - 3, 0, -1):
+                z = nt(bf(z), rv[up]) + fl[up]
+            zb1[0] = bf(z)
+            zsend = send(zb1.at[0], zb1.at[1], zs.at[0], zs.at[1], partners[0])
+            z0 = nt(zb1[0], rv[0]) + f0[1]
+            acc[1] += nt(uv[...], bf(z0))
+            zsend.wait_recv()
+            z0 = nt(zb1[1], rv[0]) + f0[0]
+            acc[0] += nt(uv[...], bf(z0))
+
     rz = []
     for k in range(CHUNKS):
         rows = pl.ds(k * step, step)
         rc[levels - 1, k].wait_recv()
-        z = nt(rcb[levels - 1, rows], bv[levels - 1])
-        for height in range(levels - 2, 0, -1):
-            z = nt(bf(z), rv[height]) + fl[height, rows]
-        zb1[rows] = bf(z)
-        rz.append(send(zb1.at[rows], rz1.at[rows], szs.at[k], rzs.at[k], partners[0]))
-    z0 = nt(zb1[...], rv[0]) + f0[1]
-    out[:, self_cols] = bf(acc[1] + nt(uv[...], bf(z0)))
+        rz.append(send(rcb.at[levels - 1, rows], rz1.at[rows], szs.at[k], rzs.at[k], partners[0]))
+    out[:, self_cols] = bf(acc[1] + nt(path[...], rcb[levels - 1]))
     for copy in rz:
         copy.wait_recv()
-    z0 = nt(rz1[...], rv[0]) + f0[0]
-    out[:, other_cols] = bf(acc[0] + nt(uv[...], bf(z0)))
+    out[:, other_cols] = bf(acc[0] + nt(path[...], rz1[...]))
     for copy in sent:
         copy.wait_send()
 
@@ -200,7 +209,7 @@
     hbm = pl.BlockSpec(memory_space=pltpu.HBM)
     return pl.pallas_call(
         functools.partial(kernel, levels, low),
-        out_shape=jax.ShapeDtypeStruct((leaf, ncol), b16),
+        out_shape=pltpu.VMEM((leaf, ncol), b16),
         in_specs=[hbm] * 10,
         out_specs=pl.BlockSpec(memory_space=pltpu.VMEM),
         scratch_shapes=[
@@ -222,8 +231,11 @@
             pltpu.VMEM((levels - 1, half, rank), f4),
             pltpu.VMEM((2, half, rank), f4),
             pltpu.VMEM((2, leaf, half), f4),
+            pltpu.VMEM((2, half, rank), b16),
             pltpu.VMEM((half, rank), b16),
-            pltpu.VMEM((half, rank), b16),
+            pltpu.VMEM((rank, rank), b16),
+            pltpu.VMEM((leaf, rank), b16),
+            dma((2,)),
             dma((4 * levels + 8,)),
             dma((2,)),
             dma((2,)),

time: 25.1 us -> 22.1 us (0.88)
  Pallas kernels: 23.1 us -> 21.1 us
  local copies, waits for them, and re-layouts: 1.67 us -> 0.71 us
    pallas_call x1, Pallas kernels: 23.1 us -> 21.1 us  [per_device(): pl.pallas_call(functools.partial(kernel, levels, low), out_shape=pltpu.VM...]
    unnamed x1, local copies, waits for them, and re-layouts: 1.67 us -> 0.71 us
where the time goes in v2:
time: 22.1 us; the launch traced here: 21.8 us
  Pallas kernels  21.1 us (95%)
  local copies, waits for them, and re-layouts  0.71 us (3%)
    pallas_call x1, Pallas kernels, per_device(): pl.pallas_call(functools.partial(kernel, levels, low), out_shape=pltpu.VM...  21.1 us
    unnamed x1, local copies, waits for them, and re-layouts  0.71 us

profile of v2, /device:TPU:0, one launch (start us, length us, event | category | flops | bytes accessed | tf_op | source)
XLA Modules:
  0.0 21.8 jit_solution(3655066932936796551)
XLA Ops:
  0.0 21.1 %shard_map.100 = bf16[512,256]{1,0:T(8,128)(2,1)S(1)} custom-call(bf16[512,256]{1,0:T(8,128)(2,1)} %x.1, bf16[512,512]{1,0:T(8,128)(2,1)} %d.1, bf16[512,256]{1,0:T(8,128)(2,1)} %u.1, bf16[512,256]{1,0:T(8,128)(2,1)} %v.1, bf16[1,2,256,256]{3,2,1,0:T(8,128)(2,1)} %lup.1, bf16[1,2,256,256]{3,2,1,0:T(8,128)(2,1)} %ldn.1, bf16[1,2,256,256]{3,2,1,0:T(8,128)(2,1)} %lcp.1, ...), custom_call_target="tpu_custom_call" | custom-call | tf_op jit(solution)/shard_map/pallas_call | solution.py:210
  21.1 0.7 %copy.12 = bf16[512,256]{1,0:T(8,128)(2,1)} copy(bf16[512,256]{1,0:T(8,128)(2,1)S(1)} %shard_map.100) | data formatting | bytes 524288
